TPU v7x, 32 devices: a 4x4x1 block of a 4x4x8 slice. The times are simulated.
32 devices in a mesh: dp: 1 (over z), ep: 32 (over y, x, core).
Axes of the slice: x: 4, y: 4, z: 1, core: 2. Of those that a mesh axis runs over, the one named last changes fastest.
The devices are a block of a 4x4x8 slice.
Arguments:
- grad_out: bfloat16 [2, 4096, 1536], P(None, ('dp', 'ep'))
- expert_out: bfloat16 [2, 4096, 6, 1536], P(None, ('dp', 'ep'))
- gate_vals: float32 [2, 4096, 6], P(None, ('dp', 'ep'))
- topk_idx: int32 [2, 4096, 6], P(None, ('dp', 'ep'))
- slot_idx: int32 [2, 4096, 6], P(None, ('dp', 'ep'))
- x_dispatch: bfloat16 [2, 64, 512, 1536], P(None, ('dp', 'ep'))
- h1_pre: bfloat16 [2, 64, 512, 512], P(None, ('dp', 'ep'))
- h3_pre: bfloat16 [2, 64, 512, 512], P(None, ('dp', 'ep'))
- w_gate: bfloat16 [64, 1536, 512], P('ep')
- w_up: bfloat16 [64, 1536, 512], P('ep')
- w_down: bfloat16 [64, 512, 1536], P('ep')
Outputs:
- output 1: bfloat16 [2, 4096, 1536], P(None, ('dp', 'ep'))
- output 2: float32 [2, 4096, 6], P(None, ('dp', 'ep'))
- output 3: float32 [64, 1536, 512], P(('dp', 'ep'))
- output 4: float32 [64, 1536, 512], P(('dp', 'ep'))
- output 5: float32 [64, 512, 1536], P(('dp', 'ep'))
All inputs are finite; a program needn't handle non-finite values.
Results may differ from a plain program's by a relative error of at most 0.00867723.
Values are sent between devices in bfloat16 or wider.
A program may use at most 768 MiB of HBM per device.

v0:
```python
import functools
import jax
import jax.numpy as jnp
from jax import lax
from jax.experimental import pallas as pl
from jax.experimental.pallas import tpu as pltpu
from jax.sharding import PartitionSpec as P

MESH = pl.DeviceIdType.MESH
BF16 = jnp.bfloat16
F32 = jnp.float32
RETURN_ORDER = ((1, 0), (3, 0), (0, 1), (0, 3), (2, 0), (0, 2), (1, 1), (3, 3), (1, 3), (3, 1),
                (2, 1), (1, 2), (2, 3), (3, 2), (2, 2))


def exchange_kernel(n_dev, side, n_micro, tokens, top_k, d_model, d_ff, capacity,
                    dy_hbm, yd_hbm, gate_ref, topk_ref, slot_ref, h1_hbm, h3_hbm, w1_hbm, w3_hbm, w2_hbm,
                    dx_ref, dg_ref, dyd_hbm, dh1_hbm, dh3_hbm, act_hbm,
                    full, leaf, sib, dyd, dxs, ret, route, pad, w1, w3, w2, h1, h3, act_v, onehot, ybuf,
                    full_recv, full_send, leaf_send, sib_send, dyd_recv, route_send, route_recv,
                    ret_send, ret_recv, load_sem, y_sem, out_sem):
    me = lax.axis_index('ep')
    core = me % 2
    chip_x = (me // 2) % side
    chip_y = me // (2 * side)
    rows_dev = 2 * capacity
    half = d_model // 2

    def device(da, db, which):
        dx = da * (1 - core) + db * core
        dy = da * core + db * (1 - core)
        return (((chip_y + dy + 2 * side) % side) * side + (chip_x + dx + 2 * side) % side) * 2 + which

    def load_own(m, h):
        return pltpu.make_async_copy(dy_hbm.at[m, :, pl.ds(h * half, half)], full.at[m, h, 0], full_recv.at[m, h, 0])

    for m in range(n_micro):
        for h in range(2):
            load_own(m, h).start()
    loads = [pltpu.make_async_copy(src, dst, load_sem.at[i]) for i, (src, dst) in enumerate(
        ((w2_hbm, w2), (h1_hbm, h1), (h3_hbm, h3), (w1_hbm, w1), (w3_hbm, w3)))]

    barrier = pltpu.get_barrier_semaphore()

    def greet(k, carry):
        pl.semaphore_signal(barrier, inc=1, device_id={'ep': (me + k) % n_dev}, device_id_type=MESH)
        return carry

    lax.fori_loop(1, n_dev, greet, 0)
    for c in loads:
        c.start()

    for m in range(n_micro):
        pad[...] = jnp.zeros_like(pad)
        key = jnp.where(slot_ref[m] >= 0, topk_ref[m] * capacity + slot_ref[m], -1)
        pad[:, 0:top_k] = key.astype(F32)
        pad[:, 8:8 + top_k] = gate_ref[m]
        route[me, m] = jnp.transpose(pad[...])[0:16, :]
    pl.semaphore_wait(barrier, n_dev - 1)

    def send_route(da, db):
        pltpu.make_async_remote_copy(route.at[me], route.at[me], route_send, route_recv,
                                     device_id={'ep': device(da, db, core)}, device_id_type=MESH).start()

    n_route = 0
    for da, db in ((1, 0), (side - 1, 0), (2, 0), (0, 1), (0, side - 1), (1, 1), (1, side - 1), (side - 1, 1),
                   (side - 1, side - 1), (2, 1), (2, side - 1)):
        send_route(da, db)
        n_route += 1

    def send_full(m, h, ev, da, db, slot):
        pltpu.make_async_remote_copy(full.at[m, h, ev], full.at[m, h, slot], full_send, full_recv.at[m, h, slot],
                                     device_id={'ep': device(da, db, core)}, device_id_type=MESH).start()

    def item(m, i):
        h = i % 2
        ev = i // 2
        s = 1 - 2 * h
        pltpu.make_async_copy(full.at[m, h, ev], full.at[m, h, ev], full_recv.at[m, h, ev]).wait()

        @pl.when(ev == 0)
        def _():
            send_full(m, h, ev, s, 0, 1)
            send_full(m, h, ev, -s, 0, 2)

        @pl.when(ev == 1)
        def _():
            send_full(m, h, ev, s, 0, 3)

        @pl.when(ev < 4)
        def _():
            send_full(m, h, ev, 0, s, 4 + ev)

        k = ev % 4
        lvl = ev // 4
        da = (k % 2) * (1 - k // 2) * (-s) + (k // 2) * (1 - k % 2) * s + (k // 2) * (k % 2) * 2
        home = device(da, -s * lvl, core)
        leaf_chip = device(0, s * (2 * lvl - 1), 0)
        row = lax.broadcasted_iota(jnp.int32, (4 * rows_dev, tokens), 0)
        block = row // rows_dev
        inner = row - block * rows_dev
        dev = jnp.where(block == 0, me, jnp.where(block == 1, me + 1 - 2 * core,
                                                  jnp.where(block == 2, leaf_chip, leaf_chip + 1)))
        want = (dev * rows_dev + inner).astype(F32)
        table = route[home, m]
        pick = jnp.zeros((4 * rows_dev, tokens), F32)
        gate = jnp.zeros((4 * rows_dev, tokens), F32)
        for j in range(top_k):
            hit = want == table[j:j + 1, :]
            pick = jnp.where(hit, 1.0, pick)
            gate = jnp.where(hit, table[8 + j:9 + j, :], gate)
        gate = jnp.sum(gate, axis=1, keepdims=True)
        rows = jnp.dot(pick.astype(BF16), full[m, h, ev], preferred_element_type=F32)
        rows = (rows * gate).astype(BF16)
        leaf[m, h, ev] = rows[2 * rows_dev:].reshape(2, 2, capacity, half)
        sib[m, h, ev] = rows[rows_dev:2 * rows_dev].reshape(2, capacity, half)
        row0 = pl.multiple_of(home * capacity, capacity)
        col0 = pl.multiple_of(h * half, half)
        dyd[m, :, pl.ds(row0, capacity), pl.ds(col0, half)] = rows[:rows_dev].reshape(2, capacity, half)
        target = dyd.at[m, :, pl.ds(row0, capacity), pl.ds(col0, half)]
        for c in range(2):
            pltpu.make_async_remote_copy(leaf.at[m, h, ev, c], target, leaf_send, dyd_recv.at[m],
                                         device_id={'ep': leaf_chip + c}, device_id_type=MESH).start()
        pltpu.make_async_remote_copy(sib.at[m, h, ev], target, sib_send, dyd_recv.at[m],
                                     device_id={'ep': me + 1 - 2 * core}, device_id_type=MESH).start()

    def items(m, lo, hi):
        lax.fori_loop(lo, hi, lambda i, c: (item(m, i), c)[1], 0)

    chunk = 256
    per_exp = (n_dev * capacity) // chunk

    def compute(m, c):
        e = c // per_exp
        r0 = pl.multiple_of((c % per_exp) * chunk, chunk)
        nt = (((1,), (1,)), ((), ()))
        grad_act = lax.dot_general(dyd[m, e, pl.ds(r0, chunk)], w2[e], nt, preferred_element_type=F32)
        grad_act = grad_act.astype(BF16).astype(F32)
        h1_f32 = h1[m, e, pl.ds(r0, chunk)].astype(F32)
        h3_f32 = h3[m, e, pl.ds(r0, chunk)].astype(F32)
        sig = jax.nn.sigmoid(h1_f32)
        silu = h1_f32 * sig
        act = (silu * h3_f32).astype(BF16)
        grad_h1 = (grad_act * h3_f32 * sig * (1.0 + h1_f32 * (1.0 - sig))).astype(BF16)
        grad_h3 = (grad_act * silu).astype(BF16)
        rows = lax.dot_general(grad_h1, w1[e], nt, preferred_element_type=F32)
        rows = rows + lax.dot_general(grad_h3, w3[e], nt, preferred_element_type=F32)
        dxs[m, e, pl.ds(r0, chunk)] = rows.astype(BF16)
        h1[m, e, pl.ds(r0, chunk)] = grad_h1
        h3[m, e, pl.ds(r0, chunk)] = grad_h3
        act_v[m, e, pl.ds(r0, chunk)] = act

    def send_return(m):
        for which in range(2):
            for dx, dy in RETURN_ORDER:
                dst = (((chip_y + dy) % side) * side + (chip_x + dx) % side) * 2 + (core + which) % 2
                send_row(m, dst)
            if which == 0:
                send_row(m, me + 1 - 2 * core)

    def send_row(m, dst):
        row0 = pl.multiple_of(dst * capacity, capacity)
        pltpu.make_async_remote_copy(dxs.at[m, :, pl.ds(row0, capacity)], ret.at[m, me], ret_send, ret_recv.at[m],
                                     device_id={'ep': dst}, device_id_type=MESH).start()

    def out_copies(m):
        return [pltpu.make_async_copy(src.at[m], dst.at[m], out_sem.at[m, i]) for i, (src, dst) in enumerate(
            ((dyd, dyd_hbm), (h1, dh1_hbm), (h3, dh3_hbm), (act_v, act_hbm)))]

    def combine(m):
        key = jnp.where(slot_ref[m] >= 0, topk_ref[m] * capacity + slot_ref[m], -1)
        lane = lax.broadcasted_iota(jnp.int32, (tokens, n_dev * rows_dev), 1)
        mat = jnp.zeros((tokens, n_dev * rows_dev), F32)
        for j in range(top_k):
            mat = jnp.where(lane == key[:, j:j + 1], 1.0, mat)
        onehot[m] = mat.astype(BF16)
        row0 = pl.multiple_of(me * capacity, capacity)
        ret[m, me] = dxs[m, :, pl.ds(row0, capacity)]
        pltpu.make_async_copy(ret.at[m, pl.ds(0, n_dev - 1)], ret.at[m, pl.ds(0, n_dev - 1)], ret_recv.at[m]).wait()
        for c in range(0, d_model, 512):
            back = ret[m, :, :, :, c:c + 512].reshape(n_dev * rows_dev, 512)
            dx_ref[m, :, c:c + 512] = jnp.dot(onehot[m], back, preferred_element_type=F32).astype(BF16)

    pltpu.make_async_copy(route.at[pl.ds(0, n_route)], route.at[pl.ds(0, n_route)], route_recv).wait()
    items(0, 0, 8)
    items(1, 0, 2)
    items(0, 8, 16)
    items(1, 2, 8)

    def wait_dyd(m):
        part = dyd.at[m, :, pl.ds(0, (n_dev - 8) * capacity)]
        pltpu.make_async_copy(part, part, dyd_recv.at[m]).wait()

    for c in loads:
        c.wait()
    wait_dyd(0)

    def mixed(c, carry):
        compute(0, c)
        item(1, 8 + 2 * c)
        item(1, 9 + 2 * c)
        return carry

    lax.fori_loop(0, 2 * per_exp, mixed, 0)
    send_return(0)
    wait_dyd(1)
    lax.fori_loop(0, 2 * per_exp, lambda c, carry: (compute(1, c), carry)[1], 0)
    send_return(1)
    outs = out_copies(0) + out_copies(1)
    for c in outs:
        c.start()

    t_blk = ybuf.shape[1]
    n_blk = tokens // t_blk

    def y_copy(i):
        m = i // n_blk
        t0 = (i % n_blk) * t_blk
        return pltpu.make_async_copy(yd_hbm.at[m, pl.ds(t0, t_blk)], ybuf.at[i % 2], y_sem.at[i % 2])

    y_copy(0).start()

    def gate_grad(i, carry):
        @pl.when(i + 1 < n_micro * n_blk)
        def _():
            y_copy(i + 1).start()

        y_copy(i).wait()
        m = i // n_blk
        t0 = pl.multiple_of((i % n_blk) * t_blk, t_blk)
        total = jnp.zeros((t_blk, top_k), F32)
        for h in range(2):
            dy_blk = full[m, h, 0, pl.ds(t0, t_blk), :].astype(F32)
            y_blk = ybuf[i % 2, :, :, h * half:(h + 1) * half].astype(F32)
            total = total + jnp.sum(y_blk * dy_blk[:, None, :], axis=-1)
        dg_ref[m, pl.ds(t0, t_blk), :] = total
        return carry

    lax.fori_loop(0, n_micro * n_blk, gate_grad, 0)
    for m in range(n_micro):
        combine(m)
    for c in outs:
        c.wait()
    sent = full.at[:, :, pl.ds(0, 7)]
    pltpu.make_async_copy(sent, sent, full_send).wait()
    pltpu.make_async_copy(leaf, leaf, leaf_send).wait()
    pltpu.make_async_copy(sib, sib, sib_send).wait()
    pltpu.make_async_copy(route.at[pl.ds(0, n_route)], route.at[pl.ds(0, n_route)], route_send).wait()
    pltpu.make_async_copy(ret.at[:, pl.ds(0, n_dev - 1)], ret.at[:, pl.ds(0, n_dev - 1)], ret_send).wait()


def solution(mesh):
    n_dev = mesh.shape['ep']
    side = 1
    while 2 * side * side < n_dev:
        side += 1
    tok_spec = P(None, ('dp', 'ep'))
    w_spec = P('ep')
    grad_w_spec = P(('dp', 'ep'))

    def local_step(grad_out, expert_out, gate_vals, topk_idx, slot_idx, x_dispatch, h1_pre, h3_pre, w_gate, w_up, w_down):
        n_micro, tokens, top_k, d_model = expert_out.shape
        local_exp, _, d_ff = w_gate.shape
        rows = x_dispatch.shape[2]
        capacity = rows // n_dev
        half = d_model // 2
        hbm = pl.BlockSpec(memory_space=pl.ANY)
        vmem = pl.BlockSpec(memory_space=pltpu.VMEM)
        dma = pltpu.SemaphoreType.DMA
        kernel = functools.partial(exchange_kernel, n_dev, side, n_micro, tokens, top_k, d_model, d_ff, capacity)
        ff_shape = (n_micro, local_exp, rows, d_ff)
        wide_shape = (n_micro, local_exp, rows, d_model)
        grad_x, grad_gate, dyd, grad_h1, grad_h3, act = pl.pallas_call(
            kernel,
            name='exchange',
            out_shape=(
                jax.ShapeDtypeStruct((n_micro, tokens, d_model), BF16),
                jax.ShapeDtypeStruct((n_micro, tokens, top_k), F32),
                jax.ShapeDtypeStruct(wide_shape, BF16),
                jax.ShapeDtypeStruct(ff_shape, BF16),
                jax.ShapeDtypeStruct(ff_shape, BF16),
                jax.ShapeDtypeStruct(ff_shape, BF16),
            ),
            in_specs=[hbm, hbm, vmem, vmem, vmem, hbm, hbm, hbm, hbm, hbm],
            out_specs=(vmem, vmem, hbm, hbm, hbm, hbm),
            scratch_shapes=[
                pltpu.VMEM((n_micro, 2, 8, tokens, half), BF16),
                pltpu.VMEM((n_micro, 2, 8, 2, local_exp, capacity, half), BF16),
                pltpu.VMEM((n_micro, 2, 8, local_exp, capacity, half), BF16),
                pltpu.VMEM(wide_shape, BF16),
                pltpu.VMEM(wide_shape, BF16),
                pltpu.VMEM((n_micro, n_dev, local_exp, capacity, d_model), BF16),
                pltpu.VMEM((n_dev, n_micro, 16, tokens), F32),
                pltpu.VMEM((tokens, 128), F32),
                pltpu.VMEM(w_gate.shape, BF16),
                pltpu.VMEM(w_up.shape, BF16),
                pltpu.VMEM(w_down.shape, BF16),
                pltpu.VMEM(ff_shape, BF16),
                pltpu.VMEM(ff_shape, BF16),
                pltpu.VMEM(ff_shape, BF16),
                pltpu.VMEM((n_micro, tokens, n_dev * local_exp * capacity), BF16),
                pltpu.VMEM((2, 16, top_k, d_model), BF16),
                dma((n_micro, 2, 8)),
                dma, dma, dma,
                dma((n_micro,)),
                dma, dma, dma,
                dma((n_micro,)),
                dma((5,)),
                dma((2,)),
                dma((n_micro, 4)),
            ],
            compiler_params=pltpu.CompilerParams(collective_id=0, has_side_effects=True, vmem_limit_bytes=67043328),
            cost_estimate=pl.CostEstimate(flops=10 ** 10, bytes_accessed=5 * 10 ** 7, transcendentals=0),
        )(grad_out, expert_out, gate_vals, topk_idx, slot_idx, h1_pre, h3_pre, w_gate, w_up, w_down)
        grad_w_gate = jnp.einsum('merd,merf->edf', x_dispatch, grad_h1, preferred_element_type=F32)
        grad_w_up = jnp.einsum('merd,merf->edf', x_dispatch, grad_h3, preferred_element_type=F32)
        grad_w_down = jnp.einsum('merf,merd->efd', act, dyd, preferred_element_type=F32)
        return grad_x, grad_gate, grad_w_gate, grad_w_up, grad_w_down

    in_specs = (tok_spec,) * 8 + (w_spec,) * 3
    out_specs = (tok_spec, tok_spec, grad_w_spec, grad_w_spec, grad_w_spec)
    return jax.shard_map(local_step, mesh=mesh, in_specs=in_specs, out_specs=out_specs, check_vma=False)
```

profile of v0, /device:TPU:97, one launch (start us, length us, event | category | flops | bytes accessed | tf_op | source)
XLA Modules:
  0.0 191.2 jit_solution(17899294474192389680)
XLA Ops:
  0.6 0.0 copy-start.2
  0.6 0.0 copy-start.3
  0.7 0.0 copy-start.4
  0.7 7.8 %copy.16.yd_hbm = bf16[2,128,6,1536]{3,2,1,0:T(8,128)(2,1)} copy(bf16[2,128,6,1536]{3,1,2,0:T(8,128)(2,1)} %param.12) | data formatting | bytes 9437184 | tf_op args[1]
  8.4 0.0 copy-done.2
  8.4 0.8 copy.17.gate_ref
  9.2 0.0 copy-done.3
  9.2 0.8 copy.18.topk_ref
  10.0 0.0 copy-done.4
  10.0 0.8 copy.19.slot_ref
  10.8 142.1 %exchange.1 = (bf16[2,128,1536]{2,1,0:T(8,128)(2,1)}, f32[2,128,6]{2,1,0:T(8,128)}, bf16[2,2,512,1536]{3,2,1,0:T(8,128)(2,1)}, bf16[2,2,512,512]{3,2,1,0:T(8,128...) custom-call(bf16[2,128,1536]{2,1,0:T(8,128)(2,1)} %dy_hbm.1, ...), custom_call_target="tpu_custom_call" | custom-call | flops 10000000000 | bytes 50000000 | tf_op jit(solution)/shard_map/exchange/pallas_call | solution.py:273
  153.0 0.0 copy-start.5
  153.0 0.0 copy-start.7
  153.0 9.7 %convolution_bitcast_fusion = f32[2,512,1536]{2,1,0:T(8,128)} fusion(bf16[2,2,512,512]{3,2,1,0:T(8,128)(2,1)} %get-tuple-element.15, bf16[2,2,512,1536]{3,2,1,0:T(8,128)(2,1)} %get-tuple-element.16), kind=kOutput, calls=%fused_computation | convolution fusion | flops 3221225472 | bytes 14680064 | tf_op jit(solution)/shard_map/merf,merd->efd/dot_general | solution.py:317
  162.7 0.0 copy-done.5
  162.7 0.0 copy-done.7
  162.7 5.4 %convolution_bitcast_fusion.2 = f32[2,1536,512]{1,2,0:T(8,128)} fusion(bf16[2,2,512,512]{3,2,1,0:T(8,128)(2,1)S(1)} %copy-done.7, bf16[2,2,512,1536]{3,2,1,0:T(8,128)(2,1)S(1)} %copy-done.5), kind=kOutput, calls=%fused_computation.2 | convolution fusion | flops 3221225472 | bytes 14680064 | tf_op jit(solution)/shard_map/merd,merf->edf/dot_general | solution.py:315
  168.1 0.0 copy-start.6
  168.1 6.7 %copy.27 = f32[2,1536,512]{2,1,0:T(8,128)} copy(f32[2,1536,512]{1,2,0:T(8,128)} %convolution_bitcast_fusion.2) | data formatting | bytes 12582912
  174.8 0.0 copy-done.6
  174.8 8.2 %convolution_bitcast_fusion.1 = f32[2,1536,512]{1,2,0:T(8,128)} fusion(bf16[2,2,512,512]{3,2,1,0:T(8,128)(2,1)S(1)} %copy-done.6, bf16[2,2,512,1536]{3,2,1,0:T(8,128)(2,1)} %param.16), kind=kOutput, calls=%fused_computation.1 | convolution fusion | flops 3221225472 | bytes 14680064 | tf_op jit(solution)/shard_map/merd,merf->edf/dot_general | solution.py:316
  183.0 0.0 copy-start.1
  183.0 0.0 copy-start
  183.0 6.6 %copy.28 = f32[2,1536,512]{2,1,0:T(8,128)} copy(f32[2,1536,512]{1,2,0:T(8,128)} %convolution_bitcast_fusion.1) | data formatting | bytes 12582912
  189.6 0.0 copy-done.1
  189.6 0.7 copy.26
  190.3 0.0 copy-done
  190.3 0.9 copy.36
Async XLA Ops:
  0.6 7.8 %copy-start.2 = (f32[2,128,6]{1,0,2:T(2,128)S(1)}, f32[2,128,6]{1,0,2:T(2,128)}, u32[]{:S(2)}) copy-start(f32[2,128,6]{1,0,2:T(2,128)} %param.13) | copy-start | bytes 18436
  0.6 8.6 %copy-start.3 = (s32[2,128,6]{1,0,2:T(2,128)S(1)}, s32[2,128,6]{1,0,2:T(2,128)}, u32[]{:S(2)}) copy-start(s32[2,128,6]{1,0,2:T(2,128)} %param.14) | copy-start | bytes 18436
  0.7 9.4 %copy-start.4 = (s32[2,128,6]{1,0,2:T(2,128)S(1)}, s32[2,128,6]{1,0,2:T(2,128)}, u32[]{:S(2)}) copy-start(s32[2,128,6]{1,0,2:T(2,128)} %param.15) | copy-start | bytes 18436
  153.0 9.8 %copy-start.5 = (bf16[2,2,512,1536]{3,2,1,0:T(8,128)(2,1)S(1)}, bf16[2,2,512,1536]{3,2,1,0:T(8,128)(2,1)}, u32[]{:S(2)}) copy-start(bf16[2,2,512,1536]{3,2,1,0:T(8,128)(2,1)} %param.16) | copy-start | bytes 18874372
  153.0 9.8 %copy-start.7 = (bf16[2,2,512,512]{3,2,1,0:T(8,128)(2,1)S(1)}, bf16[2,2,512,512]{3,2,1,0:T(8,128)(2,1)}, u32[]{:S(2)}) copy-start(bf16[2,2,512,512]{3,2,1,0:T(8,128)(2,1)} %get-tuple-element.13) | copy-start | bytes 6291460
  168.1 6.7 %copy-start.6 = (bf16[2,2,512,512]{3,2,1,0:T(8,128)(2,1)S(1)}, bf16[2,2,512,512]{3,2,1,0:T(8,128)(2,1)}, u32[]{:S(2)}) copy-start(bf16[2,2,512,512]{3,2,1,0:T(8,128)(2,1)} %get-tuple-element.14) | copy-start | bytes 6291460
  183.0 6.6 %copy-start.1 = (f32[2,128,6]{2,1,0:T(8,128)S(1)}, f32[2,128,6]{2,1,0:T(8,128)}, u32[]{:S(2)}) copy-start(f32[2,128,6]{2,1,0:T(8,128)} %get-tuple-element.18) | copy-start | bytes 18436
  183.0 7.3 %copy-start = (bf16[2,128,1536]{2,1,0:T(8,128)(2,1)S(1)}, bf16[2,128,1536]{2,1,0:T(8,128)(2,1)}, u32[]{:S(2)}) copy-start(bf16[2,128,1536]{2,1,0:T(8,128)(2,1)} %get-tuple-element.27) | copy-start | bytes 2359300
where the time goes:
time: 195 us; the launch traced here: 191 us
  Pallas kernels  142 us (73%)
  local copies, waits for them, and re-layouts  25.1 us (13%)
  matrix products  23.3 us (12%)
    pallas_call x1, Pallas kernels, local_step(): pl.pallas_call(kernel, name='exchange', out_shape=(jax.ShapeDtypeStruct((...  142 us
    unnamed x24, local copies, waits for them, and re-layouts  25.1 us
    dot_general x1, matrix products, local_step(): jnp.einsum('merf,merd->efd', act, dyd, preferred_element_type=F32)  9.73 us
    dot_general x1, matrix products, local_step(): jnp.einsum('merd,merf->edf', x_dispatch, grad_h3, preferred_element_type=...  8.17 us
    dot_general x1, matrix products, local_step(): jnp.einsum('merd,merf->edf', x_dispatch, grad_h1, preferred_element_type=...  5.37 us

commit v1 on v0

--- a/solution.py
+++ b/solution.py
@@ -51,11 +51,11 @@
         c.start()
 
     for m in range(n_micro):
-        pad[...] = jnp.zeros_like(pad)
-        key = jnp.where(slot_ref[m] >= 0, topk_ref[m] * capacity + slot_ref[m], -1)
-        pad[:, 0:top_k] = key.astype(F32)
-        pad[:, 8:8 + top_k] = gate_ref[m]
-        route[me, m] = jnp.transpose(pad[...])[0:16, :]
+        slot = slot_ref[:, m, :]
+        key = jnp.where(slot >= 0, topk_ref[:, m, :] * capacity + slot, -1)
+        route[me, m] = jnp.zeros((16, tokens), F32)
+        route[me, m, 0:top_k] = key.astype(F32)
+        route[me, m, 8:8 + top_k] = gate_ref[:, m, :]
     pl.semaphore_wait(barrier, n_dev - 1)
 
     def send_route(da, db):
@@ -168,11 +168,13 @@
             ((dyd, dyd_hbm), (h1, dh1_hbm), (h3, dh3_hbm), (act_v, act_hbm)))]
 
     def combine(m):
-        key = jnp.where(slot_ref[m] >= 0, topk_ref[m] * capacity + slot_ref[m], -1)
-        lane = lax.broadcasted_iota(jnp.int32, (tokens, n_dev * rows_dev), 1)
+        pad[...] = jnp.zeros_like(pad)
+        pad[0:16] = route[me, m]
+        key = jnp.transpose(pad[...])
+        place = lax.broadcasted_iota(jnp.int32, (tokens, n_dev * rows_dev), 1).astype(F32)
         mat = jnp.zeros((tokens, n_dev * rows_dev), F32)
         for j in range(top_k):
-            mat = jnp.where(lane == key[:, j:j + 1], 1.0, mat)
+            mat = jnp.where(place == key[:, j:j + 1], 1.0, mat)
         onehot[m] = mat.astype(BF16)
         row0 = pl.multiple_of(me * capacity, capacity)
         ret[m, me] = dxs[m, :, pl.ds(row0, capacity)]
@@ -210,33 +212,28 @@
     for c in outs:
         c.start()
 
-    t_blk = ybuf.shape[1]
-    n_blk = tokens // t_blk
-
     def y_copy(i):
-        m = i // n_blk
-        t0 = (i % n_blk) * t_blk
-        return pltpu.make_async_copy(yd_hbm.at[m, pl.ds(t0, t_blk)], ybuf.at[i % 2], y_sem.at[i % 2])
+        return pltpu.make_async_copy(yd_hbm.at[i // top_k, i % top_k], ybuf.at[i % 2], y_sem.at[i % 2])
 
     y_copy(0).start()
-
-    def gate_grad(i, carry):
-        @pl.when(i + 1 < n_micro * n_blk)
-        def _():
-            y_copy(i + 1).start()
-
-        y_copy(i).wait()
-        m = i // n_blk
-        t0 = pl.multiple_of((i % n_blk) * t_blk, t_blk)
-        total = jnp.zeros((t_blk, top_k), F32)
-        for h in range(2):
-            dy_blk = full[m, h, 0, pl.ds(t0, t_blk), :].astype(F32)
-            y_blk = ybuf[i % 2, :, :, h * half:(h + 1) * half].astype(F32)
-            total = total + jnp.sum(y_blk * dy_blk[:, None, :], axis=-1)
-        dg_ref[m, pl.ds(t0, t_blk), :] = total
-        return carry
-
-    lax.fori_loop(0, n_micro * n_blk, gate_grad, 0)
+    lane = lax.broadcasted_iota(jnp.int32, (tokens, 128), 1)
+    for m in range(n_micro):
+        def gate_grad(j, total, m=m):
+            i = m * top_k + j
+
+            @pl.when(i + 1 < n_micro * top_k)
+            def _():
+                y_copy(i + 1).start()
+
+            y_copy(i).wait()
+            part = jnp.zeros((tokens, 128), F32)
+            for c in range(0, d_model, 128):
+                dy_blk = full[m, c // half, 0, :, c % half:c % half + 128].astype(F32)
+                part = part + dy_blk * ybuf[i % 2, :, c:c + 128].astype(F32)
+            return jnp.where(lane == j, jnp.sum(part, axis=1, keepdims=True), total)
+
+        total = lax.fori_loop(0, top_k, gate_grad, jnp.zeros((tokens, 128), F32))
+        dg_ref[:, m, :] = jnp.transpose(total)[0:top_k, :]
     for m in range(n_micro):
         combine(m)
     for c in outs:
@@ -249,6 +246,37 @@
     pltpu.make_async_copy(ret.at[:, pl.ds(0, n_dev - 1)], ret.at[:, pl.ds(0, n_dev - 1)], ret_send).wait()
 
 
+def weight_kernel(x_ref, g1_ref, g3_ref, act_ref, dy_ref, o1_ref, o3_ref, o2_ref):
+    tn = (((0,), (0,)), ((), ()))
+
+    def flat(ref):
+        return ref[...].reshape(-1, ref.shape[-1])
+
+    x = flat(x_ref)
+    o1_ref[0] = lax.dot_general(x, flat(g1_ref), tn, preferred_element_type=F32)
+    o3_ref[0] = lax.dot_general(x, flat(g3_ref), tn, preferred_element_type=F32)
+    o2_ref[0] = lax.dot_general(flat(act_ref), flat(dy_ref), tn, preferred_element_type=F32)
+
+
+def weight_grads(x, g1, g3, act, dy):
+    n_micro, local_exp, rows, d_model = x.shape
+    d_ff = g1.shape[-1]
+    tile = 256
+    wide = pl.BlockSpec((n_micro, 1, rows, tile), lambda e, t: (0, e, 0, t))
+    narrow = pl.BlockSpec((n_micro, 1, rows, d_ff), lambda e, t: (0, e, 0, 0))
+    tall = pl.BlockSpec((1, tile, d_ff), lambda e, t: (e, t, 0))
+    return pl.pallas_call(
+        weight_kernel,
+        name='weight_grads',
+        grid=(local_exp, d_model // tile),
+        out_shape=(jax.ShapeDtypeStruct((local_exp, d_model, d_ff), F32),) * 2
+        + (jax.ShapeDtypeStruct((local_exp, d_ff, d_model), F32),),
+        in_specs=[wide, narrow, narrow, narrow, wide],
+        out_specs=(tall, tall, pl.BlockSpec((1, d_ff, tile), lambda e, t: (e, 0, t))),
+        compiler_params=pltpu.CompilerParams(vmem_limit_bytes=67043328),
+    )(x, g1, g3, act, dy)
+
+
 def solution(mesh):
     n_dev = mesh.shape['ep']
     side = 1
@@ -265,6 +293,7 @@
         capacity = rows // n_dev
         half = d_model // 2
         hbm = pl.BlockSpec(memory_space=pl.ANY)
+        by_choice = functools.partial(jnp.transpose, axes=(2, 0, 1))
         vmem = pl.BlockSpec(memory_space=pltpu.VMEM)
         dma = pltpu.SemaphoreType.DMA
         kernel = functools.partial(exchange_kernel, n_dev, side, n_micro, tokens, top_k, d_model, d_ff, capacity)
@@ -275,7 +304,7 @@
             name='exchange',
             out_shape=(
                 jax.ShapeDtypeStruct((n_micro, tokens, d_model), BF16),
-                jax.ShapeDtypeStruct((n_micro, tokens, top_k), F32),
+                jax.ShapeDtypeStruct((top_k, n_micro, tokens), F32),
                 jax.ShapeDtypeStruct(wide_shape, BF16),
                 jax.ShapeDtypeStruct(ff_shape, BF16),
                 jax.ShapeDtypeStruct(ff_shape, BF16),
@@ -299,7 +328,7 @@
                 pltpu.VMEM(ff_shape, BF16),
                 pltpu.VMEM(ff_shape, BF16),
                 pltpu.VMEM((n_micro, tokens, n_dev * local_exp * capacity), BF16),
-                pltpu.VMEM((2, 16, top_k, d_model), BF16),
+                pltpu.VMEM((2, tokens, d_model), BF16),
                 dma((n_micro, 2, 8)),
                 dma, dma, dma,
                 dma((n_micro,)),
@@ -311,10 +340,10 @@
             ],
             compiler_params=pltpu.CompilerParams(collective_id=0, has_side_effects=True, vmem_limit_bytes=67043328),
             cost_estimate=pl.CostEstimate(flops=10 ** 10, bytes_accessed=5 * 10 ** 7, transcendentals=0),
-        )(grad_out, expert_out, gate_vals, topk_idx, slot_idx, h1_pre, h3_pre, w_gate, w_up, w_down)
-        grad_w_gate = jnp.einsum('merd,merf->edf', x_dispatch, grad_h1, preferred_element_type=F32)
-        grad_w_up = jnp.einsum('merd,merf->edf', x_dispatch, grad_h3, preferred_element_type=F32)
-        grad_w_down = jnp.einsum('merf,merd->efd', act, dyd, preferred_element_type=F32)
+        )(grad_out, jnp.transpose(expert_out, (0, 2, 1, 3)), by_choice(gate_vals), by_choice(topk_idx), by_choice(slot_idx),
+          h1_pre, h3_pre, w_gate, w_up, w_down)
+        grad_gate = jnp.transpose(grad_gate, (1, 2, 0))
+        grad_w_gate, grad_w_up, grad_w_down = weight_grads(x_dispatch, grad_h1, grad_h3, act, dyd)
         return grad_x, grad_gate, grad_w_gate, grad_w_up, grad_w_down
 
     in_specs = (tok_spec,) * 8 + (w_spec,) * 3

time: 195 us -> 167 us (0.86); the launches traced: 191 us -> 165 us
  matrix products: 23.3 us -> 0 us
  local copies, waits for them, and re-layouts: 25.1 us -> 3.35 us
  Pallas kernels: 142 us -> 161 us
    dot_general x3 -> x0, matrix products: 23.3 us -> none  [the longest x1 9.73 us: local_step(): jnp.einsum('merf,merd->efd', act, dyd, preferred_element_type=F32)]
    unnamed x24 -> x2, local copies, waits for them, and re-layouts: 25.1 us -> 3.35 us
    pallas_call x0 -> x1, Pallas kernels: none -> 19.5 us  [weight_grads(): pl.pallas_call(weight_kernel, name='weight_grads', grid=(local_exp, d_mod...]
where the time goes in v1:
time: 167 us; the launch traced here: 165 us
  Pallas kernels  161 us (96%)
  local copies, waits for them, and re-layouts  3.35 us (2%)
    pallas_call x1, Pallas kernels, local_step(): pl.pallas_call(kernel, name='exchange', out_shape=(jax.ShapeDtypeStruct((...  142 us
    pallas_call x1, Pallas kernels, weight_grads(): pl.pallas_call(weight_kernel, name='weight_grads', grid=(local_exp, d_mod...  19.5 us
    unnamed x2, local copies, waits for them, and re-layouts  3.35 us

profile of v1, /device:TPU:97, one launch (start us, length us, event | category | flops | bytes accessed | tf_op | source)
XLA Modules:
  0.0 165.5 jit_solution(16493453878268193257)
XLA Ops:
  0.6 142.0 %exchange.1 = (bf16[2,128,1536]{2,1,0:T(8,128)(2,1)}, f32[6,2,128]{2,1,0:T(2,128)}, bf16[2,2,512,1536]{3,2,1,0:T(8,128)(2,1)}, bf16[2,2,512,512]{3,2,1,0:T(8,128...) custom-call(bf16[2,128,1536]{2,1,0:T(8,128)(2,1)} %dy_hbm.1, ...), custom_call_target="tpu_custom_call" | custom-call | flops 10000000000 | bytes 50000000 | tf_op jit(solution)/shard_map/exchange/pallas_call | solution.py:302
  142.6 19.5 %weight_grads.1 = (f32[2,1536,512]{2,1,0:T(8,128)}, f32[2,1536,512]{2,1,0:T(8,128)}, f32[2,512,1536]{2,1,0:T(8,128)}) custom-call(bf16[2,2,512,1536]{3,2,1,0:T(8,128)(2,1)} %x_ref.1, bf16[2,2,512,512]{3,2,1,0:T(8,128)(2,1)} %get-tuple-element.16.g1_ref, bf16[2,2,512,512]{3,2,1,0:T(8,128)(2,1)} %get-tuple-element.17.g3_ref, ...), custom_call_target="tpu_custom_call" | custom-call | tf_op jit(solution)/shard_map/weight_grads/pallas_call | solution.py:268
  162.1 2.1 %copy.18 = bf16[2,128,1536]{2,1,0:T(8,128)(2,1)} copy(bf16[2,128,1536]{2,1,0:T(8,128)(2,1)} %get-tuple-element.28) | data formatting | bytes 1572864
  164.2 1.3 copy.19

commit v2 on v1

--- a/solution.py
+++ b/solution.py
@@ -8,17 +8,18 @@
 
 MESH = pl.DeviceIdType.MESH
 BF16 = jnp.bfloat16
+VMEM_GRANT = 67043328 - 19 * 2 ** 20
 F32 = jnp.float32
 RETURN_ORDER = ((1, 0), (3, 0), (0, 1), (0, 3), (2, 0), (0, 2), (1, 1), (3, 3), (1, 3), (3, 1),
                 (2, 1), (1, 2), (2, 3), (3, 2), (2, 2))
 
 
 def exchange_kernel(n_dev, side, n_micro, tokens, top_k, d_model, d_ff, capacity,
-                    dy_hbm, yd_hbm, gate_ref, topk_ref, slot_ref, h1_hbm, h3_hbm, w1_hbm, w3_hbm, w2_hbm,
-                    dx_ref, dg_ref, dyd_hbm, dh1_hbm, dh3_hbm, act_hbm,
-                    full, leaf, sib, dyd, dxs, ret, route, pad, w1, w3, w2, h1, h3, act_v, onehot, ybuf,
+                    dy_hbm, yd_hbm, gate_ref, topk_ref, slot_ref, x_hbm, h1_hbm, h3_hbm, w1_hbm, w3_hbm, w2_hbm,
+                    dx_ref, dg_ref, dw1_ref, dw3_ref, dw2_ref,
+                    full, leaf, sib, dyd, dxs, ret, route, pad, w1, w3, w2, h1, h3, act_v, onehot,
                     full_recv, full_send, leaf_send, sib_send, dyd_recv, route_send, route_recv,
-                    ret_send, ret_recv, load_sem, y_sem, out_sem):
+                    ret_send, ret_recv, load_sem, y_sem, x_sem):
     me = lax.axis_index('ep')
     core = me % 2
     chip_x = (me // 2) % side
@@ -32,7 +33,7 @@
         return (((chip_y + dy + 2 * side) % side) * side + (chip_x + dx + 2 * side) % side) * 2 + which
 
     def load_own(m, h):
-        return pltpu.make_async_copy(dy_hbm.at[m, :, pl.ds(h * half, half)], full.at[m, h, 0], full_recv.at[m, h, 0])
+        return pltpu.make_async_copy(dy_hbm.at[m, :, pl.ds(h * half, half)], full.at[m, h, 0, 0], full_recv.at[m, h, 0])
 
     for m in range(n_micro):
         for h in range(2):
@@ -69,14 +70,18 @@
         n_route += 1
 
     def send_full(m, h, ev, da, db, slot):
-        pltpu.make_async_remote_copy(full.at[m, h, ev], full.at[m, h, slot], full_send, full_recv.at[m, h, slot],
+        pltpu.make_async_remote_copy(full.at[m, h, ev // 4, ev % 4], full.at[m, h, slot // 4, slot % 4],
+                                     full_send.at[m], full_recv.at[m, h, slot],
                                      device_id={'ep': device(da, db, core)}, device_id_type=MESH).start()
 
     def item(m, i):
         h = i % 2
         ev = i // 2
         s = 1 - 2 * h
-        pltpu.make_async_copy(full.at[m, h, ev], full.at[m, h, ev], full_recv.at[m, h, ev]).wait()
+        k = ev % 4
+        lvl = ev // 4
+        tok = full.at[m, h, lvl, k]
+        pltpu.make_async_copy(tok, tok, full_recv.at[m, h, ev]).wait()
 
         @pl.when(ev == 0)
         def _():
@@ -91,8 +96,6 @@
         def _():
             send_full(m, h, ev, 0, s, 4 + ev)
 
-        k = ev % 4
-        lvl = ev // 4
         da = (k % 2) * (1 - k // 2) * (-s) + (k // 2) * (1 - k % 2) * s + (k // 2) * (k % 2) * 2
         home = device(da, -s * lvl, core)
         leaf_chip = device(0, s * (2 * lvl - 1), 0)
@@ -110,7 +113,7 @@
             pick = jnp.where(hit, 1.0, pick)
             gate = jnp.where(hit, table[8 + j:9 + j, :], gate)
         gate = jnp.sum(gate, axis=1, keepdims=True)
-        rows = jnp.dot(pick.astype(BF16), full[m, h, ev], preferred_element_type=F32)
+        rows = jnp.dot(pick.astype(BF16), tok[...], preferred_element_type=F32)
         rows = (rows * gate).astype(BF16)
         leaf[m, h, ev] = rows[2 * rows_dev:].reshape(2, 2, capacity, half)
         sib[m, h, ev] = rows[rows_dev:2 * rows_dev].reshape(2, capacity, half)
@@ -129,6 +132,13 @@
 
     chunk = 256
     per_exp = (n_dev * capacity) // chunk
+
+    def out_rows(m):
+        return dxs if m == 0 else full.at[0]
+
+    def own_rows(m, dst):
+        row0 = pl.multiple_of((dst % (tokens // capacity)) * capacity, capacity)
+        return out_rows(m).at[:, :, dst // (tokens // capacity), pl.ds(row0, capacity), :]
 
     def compute(m, c):
         e = c // per_exp
@@ -145,7 +155,10 @@
         grad_h3 = (grad_act * silu).astype(BF16)
         rows = lax.dot_general(grad_h1, w1[e], nt, preferred_element_type=F32)
         rows = rows + lax.dot_general(grad_h3, w3[e], nt, preferred_element_type=F32)
-        dxs[m, e, pl.ds(r0, chunk)] = rows.astype(BF16)
+        rows = rows.astype(BF16)
+        blk = (c % per_exp) * (chunk // tokens)
+        for h in range(2):
+            out_rows(m)[h, e, pl.ds(blk, chunk // tokens)] = rows[:, h * half:(h + 1) * half].reshape(-1, tokens, half)
         h1[m, e, pl.ds(r0, chunk)] = grad_h1
         h3[m, e, pl.ds(r0, chunk)] = grad_h3
         act_v[m, e, pl.ds(r0, chunk)] = act
@@ -159,13 +172,8 @@
                 send_row(m, me + 1 - 2 * core)
 
     def send_row(m, dst):
-        row0 = pl.multiple_of(dst * capacity, capacity)
-        pltpu.make_async_remote_copy(dxs.at[m, :, pl.ds(row0, capacity)], ret.at[m, me], ret_send, ret_recv.at[m],
+        pltpu.make_async_remote_copy(own_rows(m, dst), ret.at[m, me], ret_send, ret_recv.at[m],
                                      device_id={'ep': dst}, device_id_type=MESH).start()
-
-    def out_copies(m):
-        return [pltpu.make_async_copy(src.at[m], dst.at[m], out_sem.at[m, i]) for i, (src, dst) in enumerate(
-            ((dyd, dyd_hbm), (h1, dh1_hbm), (h3, dh3_hbm), (act_v, act_hbm)))]
 
     def combine(m):
         pad[...] = jnp.zeros_like(pad)
@@ -176,12 +184,11 @@
         for j in range(top_k):
             mat = jnp.where(place == key[:, j:j + 1], 1.0, mat)
         onehot[m] = mat.astype(BF16)
-        row0 = pl.multiple_of(me * capacity, capacity)
-        ret[m, me] = dxs[m, :, pl.ds(row0, capacity)]
+        ret[m, me] = own_rows(m, me)[...]
         pltpu.make_async_copy(ret.at[m, pl.ds(0, n_dev - 1)], ret.at[m, pl.ds(0, n_dev - 1)], ret_recv.at[m]).wait()
-        for c in range(0, d_model, 512):
-            back = ret[m, :, :, :, c:c + 512].reshape(n_dev * rows_dev, 512)
-            dx_ref[m, :, c:c + 512] = jnp.dot(onehot[m], back, preferred_element_type=F32).astype(BF16)
+        for h in range(2):
+            back = ret[m, :, h].reshape(n_dev * rows_dev, half)
+            dx_ref[m, :, h * half:(h + 1) * half] = jnp.dot(onehot[m], back, preferred_element_type=F32).astype(BF16)
 
     pltpu.make_async_copy(route.at[pl.ds(0, n_route)], route.at[pl.ds(0, n_route)], route_recv).wait()
     items(0, 0, 8)
@@ -189,6 +196,9 @@
     items(0, 8, 16)
     items(1, 2, 8)
 
+    def sent_part(m):
+        return full.at[m, :, :, :, pl.ds(0, 7 * tokens // 8), :]
+
     def wait_dyd(m):
         part = dyd.at[m, :, pl.ds(0, (n_dev - 8) * capacity)]
         pltpu.make_async_copy(part, part, dyd_recv.at[m]).wait()
@@ -206,16 +216,56 @@
     lax.fori_loop(0, 2 * per_exp, mixed, 0)
     send_return(0)
     wait_dyd(1)
+    pltpu.make_async_copy(sent_part(0), sent_part(0), full_send.at[0]).wait()
     lax.fori_loop(0, 2 * per_exp, lambda c, carry: (compute(1, c), carry)[1], 0)
     send_return(1)
-    outs = out_copies(0) + out_copies(1)
-    for c in outs:
-        c.start()
+
+    tile = d_ff // 2
+    n_tile = d_model // tile
+    rows_exp = n_dev * capacity
+
+    def x_copy(i, m):
+        col = pl.multiple_of((i % n_tile) * tile, tile)
+        return pltpu.make_async_copy(x_hbm.at[m, i // n_tile, :, pl.ds(col, tile)],
+                                     w1.at[i % 2, pl.ds(m * rows_exp, rows_exp), pl.ds(0, tile)], x_sem.at[i % 2, m])
+
+    def dy_block(m):
+        return w2.at[0, pl.ds((2 + m) * tokens, tokens), :]
 
     def y_copy(i):
-        return pltpu.make_async_copy(yd_hbm.at[i // top_k, i % top_k], ybuf.at[i % 2], y_sem.at[i % 2])
-
+        return pltpu.make_async_copy(yd_hbm.at[i // top_k, i % top_k],
+                                     w2.at[0, pl.ds(pl.multiple_of((i % 2) * tokens, tokens), tokens), :], y_sem.at[i % 2])
+
+    dy_loads = [pltpu.make_async_copy(dy_hbm.at[m], dy_block(m), load_sem.at[m]) for m in range(n_micro)]
+    for m in range(n_micro):
+        x_copy(0, m).start()
+        dy_loads[m].start()
     y_copy(0).start()
+
+    def weight_step(i, carry):
+        @pl.when(i + 1 < 2 * n_tile)
+        def _():
+            for m in range(n_micro):
+                x_copy(i + 1, m).start()
+
+        for m in range(n_micro):
+            x_copy(i, m).wait()
+        e = i // n_tile
+        col = pl.multiple_of((i % n_tile) * tile, tile)
+        tn = (((0,), (0,)), ((), ()))
+        x_blk = w1[i % 2, 0:n_micro * rows_exp, 0:tile]
+        g1 = h1[:, e].reshape(n_micro * rows_exp, d_ff)
+        g3 = h3[:, e].reshape(n_micro * rows_exp, d_ff)
+        act = act_v[:, e].reshape(n_micro * rows_exp, d_ff)
+        dy_blk = dyd[:, e, :, pl.ds(col, tile)].reshape(n_micro * rows_exp, tile)
+        dw1_ref[e, pl.ds(col, tile), :] = lax.dot_general(x_blk, g1, tn, preferred_element_type=F32)
+        dw3_ref[e, pl.ds(col, tile), :] = lax.dot_general(x_blk, g3, tn, preferred_element_type=F32)
+        dw2_ref[e, :, pl.ds(col, tile)] = lax.dot_general(act, dy_blk, tn, preferred_element_type=F32)
+        return carry
+
+    lax.fori_loop(0, 2 * n_tile, weight_step, 0)
+    for c in dy_loads:
+        c.wait()
     lane = lax.broadcasted_iota(jnp.int32, (tokens, 128), 1)
     for m in range(n_micro):
         def gate_grad(j, total, m=m):
@@ -228,53 +278,19 @@
             y_copy(i).wait()
             part = jnp.zeros((tokens, 128), F32)
             for c in range(0, d_model, 128):
-                dy_blk = full[m, c // half, 0, :, c % half:c % half + 128].astype(F32)
-                part = part + dy_blk * ybuf[i % 2, :, c:c + 128].astype(F32)
+                dy_blk = w2[0, (2 + m) * tokens:(3 + m) * tokens, c:c + 128].astype(F32)
+                part = part + dy_blk * w2[0, pl.ds(pl.multiple_of((i % 2) * tokens, tokens), tokens), c:c + 128].astype(F32)
             return jnp.where(lane == j, jnp.sum(part, axis=1, keepdims=True), total)
 
         total = lax.fori_loop(0, top_k, gate_grad, jnp.zeros((tokens, 128), F32))
         dg_ref[:, m, :] = jnp.transpose(total)[0:top_k, :]
     for m in range(n_micro):
         combine(m)
-    for c in outs:
-        c.wait()
-    sent = full.at[:, :, pl.ds(0, 7)]
-    pltpu.make_async_copy(sent, sent, full_send).wait()
+    pltpu.make_async_copy(sent_part(1), sent_part(1), full_send.at[1]).wait()
     pltpu.make_async_copy(leaf, leaf, leaf_send).wait()
     pltpu.make_async_copy(sib, sib, sib_send).wait()
     pltpu.make_async_copy(route.at[pl.ds(0, n_route)], route.at[pl.ds(0, n_route)], route_send).wait()
     pltpu.make_async_copy(ret.at[:, pl.ds(0, n_dev - 1)], ret.at[:, pl.ds(0, n_dev - 1)], ret_send).wait()
-
-
-def weight_kernel(x_ref, g1_ref, g3_ref, act_ref, dy_ref, o1_ref, o3_ref, o2_ref):
-    tn = (((0,), (0,)), ((), ()))
-
-    def flat(ref):
-        return ref[...].reshape(-1, ref.shape[-1])
-
-    x = flat(x_ref)
-    o1_ref[0] = lax.dot_general(x, flat(g1_ref), tn, preferred_element_type=F32)
-    o3_ref[0] = lax.dot_general(x, flat(g3_ref), tn, preferred_element_type=F32)
-    o2_ref[0] = lax.dot_general(flat(act_ref), flat(dy_ref), tn, preferred_element_type=F32)
-
-
-def weight_grads(x, g1, g3, act, dy):
-    n_micro, local_exp, rows, d_model = x.shape
-    d_ff = g1.shape[-1]
-    tile = 256
-    wide = pl.BlockSpec((n_micro, 1, rows, tile), lambda e, t: (0, e, 0, t))
-    narrow = pl.BlockSpec((n_micro, 1, rows, d_ff), lambda e, t: (0, e, 0, 0))
-    tall = pl.BlockSpec((1, tile, d_ff), lambda e, t: (e, t, 0))
-    return pl.pallas_call(
-        weight_kernel,
-        name='weight_grads',
-        grid=(local_exp, d_model // tile),
-        out_shape=(jax.ShapeDtypeStruct((local_exp, d_model, d_ff), F32),) * 2
-        + (jax.ShapeDtypeStruct((local_exp, d_ff, d_model), F32),),
-        in_specs=[wide, narrow, narrow, narrow, wide],
-        out_specs=(tall, tall, pl.BlockSpec((1, d_ff, tile), lambda e, t: (e, 0, t))),
-        compiler_params=pltpu.CompilerParams(vmem_limit_bytes=67043328),
-    )(x, g1, g3, act, dy)
 
 
 def solution(mesh):
@@ -299,26 +315,26 @@
         kernel = functools.partial(exchange_kernel, n_dev, side, n_micro, tokens, top_k, d_model, d_ff, capacity)
         ff_shape = (n_micro, local_exp, rows, d_ff)
         wide_shape = (n_micro, local_exp, rows, d_model)
-        grad_x, grad_gate, dyd, grad_h1, grad_h3, act = pl.pallas_call(
+        out_vmem = pltpu.VMEM
+        grad_x, grad_gate, grad_w_gate, grad_w_up, grad_w_down = pl.pallas_call(
             kernel,
             name='exchange',
             out_shape=(
-                jax.ShapeDtypeStruct((n_micro, tokens, d_model), BF16),
-                jax.ShapeDtypeStruct((top_k, n_micro, tokens), F32),
-                jax.ShapeDtypeStruct(wide_shape, BF16),
-                jax.ShapeDtypeStruct(ff_shape, BF16),
-                jax.ShapeDtypeStruct(ff_shape, BF16),
-                jax.ShapeDtypeStruct(ff_shape, BF16),
+                out_vmem((n_micro, tokens, d_model), BF16),
+                out_vmem((top_k, n_micro, tokens), F32),
+                out_vmem(w_gate.shape, F32),
+                out_vmem(w_up.shape, F32),
+                out_vmem(w_down.shape, F32),
             ),
-            in_specs=[hbm, hbm, vmem, vmem, vmem, hbm, hbm, hbm, hbm, hbm],
-            out_specs=(vmem, vmem, hbm, hbm, hbm, hbm),
+            in_specs=[hbm, hbm, vmem, vmem, vmem, hbm, hbm, hbm, hbm, hbm, hbm],
+            out_specs=(vmem,) * 5,
             scratch_shapes=[
-                pltpu.VMEM((n_micro, 2, 8, tokens, half), BF16),
+                pltpu.VMEM((n_micro, 2, 2, 4, tokens, half), BF16),
                 pltpu.VMEM((n_micro, 2, 8, 2, local_exp, capacity, half), BF16),
                 pltpu.VMEM((n_micro, 2, 8, local_exp, capacity, half), BF16),
                 pltpu.VMEM(wide_shape, BF16),
-                pltpu.VMEM(wide_shape, BF16),
-                pltpu.VMEM((n_micro, n_dev, local_exp, capacity, d_model), BF16),
+                pltpu.VMEM((2, local_exp, rows // tokens, tokens, half), BF16),
+                pltpu.VMEM((n_micro, n_dev, 2, local_exp, capacity, half), BF16),
                 pltpu.VMEM((n_dev, n_micro, 16, tokens), F32),
                 pltpu.VMEM((tokens, 128), F32),
                 pltpu.VMEM(w_gate.shape, BF16),
@@ -328,22 +344,21 @@
                 pltpu.VMEM(ff_shape, BF16),
                 pltpu.VMEM(ff_shape, BF16),
                 pltpu.VMEM((n_micro, tokens, n_dev * local_exp * capacity), BF16),
-                pltpu.VMEM((2, tokens, d_model), BF16),
                 dma((n_micro, 2, 8)),
-                dma, dma, dma,
+                dma((n_micro,)),
+                dma, dma,
                 dma((n_micro,)),
                 dma, dma, dma,
                 dma((n_micro,)),
                 dma((5,)),
                 dma((2,)),
-                dma((n_micro, 4)),
+                dma((2, n_micro)),
             ],
-            compiler_params=pltpu.CompilerParams(collective_id=0, has_side_effects=True, vmem_limit_bytes=67043328),
+            compiler_params=pltpu.CompilerParams(collective_id=0, has_side_effects=True, vmem_limit_bytes=VMEM_GRANT),
             cost_estimate=pl.CostEstimate(flops=10 ** 10, bytes_accessed=5 * 10 ** 7, transcendentals=0),
         )(grad_out, jnp.transpose(expert_out, (0, 2, 1, 3)), by_choice(gate_vals), by_choice(topk_idx), by_choice(slot_idx),
-          h1_pre, h3_pre, w_gate, w_up, w_down)
+          x_dispatch, h1_pre, h3_pre, w_gate, w_up, w_down)
         grad_gate = jnp.transpose(grad_gate, (1, 2, 0))
-        grad_w_gate, grad_w_up, grad_w_down = weight_grads(x_dispatch, grad_h1, grad_h3, act, dyd)
         return grad_x, grad_gate, grad_w_gate, grad_w_up, grad_w_down
 
     in_specs = (tok_spec,) * 8 + (w_spec,) * 3

time: 167 us -> 157 us (0.940)
  the two profiles are of different devices: /device:TPU:97 before, /device:TPU:125 now
where the time goes in v2:
time: 157 us
  Pallas kernels  146 us (93%)
  local copies, waits for them, and re-layouts  9.58 us (6%)
    pallas_call x1, Pallas kernels, local_step(): pl.pallas_call(kernel, name='exchange', out_shape=(out_vmem((n_micro, tok...  146 us
    unnamed x5, local copies, waits for them, and re-layouts  9.58 us

profile of v2, /device:TPU:125, one launch (start us, length us, event | category | flops | bytes accessed | tf_op | source)
XLA Modules:
  0.0 156.7 jit_solution(2021616312595592893)
XLA Ops:
  0.6 146.5 %exchange.1 = (bf16[2,128,1536]{2,1,0:T(8,128)(2,1)S(1)}, f32[6,2,128]{2,1,0:T(2,128)S(1)}, f32[2,1536,512]{2,1,0:T(8,128)S(1)}, f32[2,1536,512]{2,1,0:T(8,128)S(1)}, f32[2,512,1536]{2,1,0:T(8,128)S(1)}) custom-call(bf16[2,128,1536]{2,1,0:T(8,128)(2,1)} %dy_hbm.1, bf16[2,6,128,1536]{3,2,1,0:T(8,128)(2,1)} %bitcast.6, f32[6,2,128]{2,1,0:T(2,128)} %bitcast.7, ...), custom_call_target="tpu_custom_call" | custom-call | flops 10000000000 | bytes 50000000 | tf_op jit(solution)/shard_map/exchange/pallas_call | solution.py:319
  147.1 0.9 copy.21
  148.0 0.6 copy.22
  148.6 2.7 %copy.23 = f32[2,1536,512]{2,1,0:T(8,128)} copy(f32[2,1536,512]{2,1,0:T(8,128)S(1)} %get-tuple-element.17) | data formatting | bytes 12582912
  151.3 2.7 %copy.24 = f32[2,1536,512]{2,1,0:T(8,128)} copy(f32[2,1536,512]{2,1,0:T(8,128)S(1)} %get-tuple-element.18) | data formatting | bytes 12582912
  154.0 2.7 %copy.25 = f32[2,512,1536]{2,1,0:T(8,128)} copy(f32[2,512,1536]{2,1,0:T(8,128)S(1)} %get-tuple-element.19) | data formatting | bytes 12582912

commit v3 on v2

--- a/solution.py
+++ b/solution.py
@@ -8,18 +8,15 @@
 
 MESH = pl.DeviceIdType.MESH
 BF16 = jnp.bfloat16
-VMEM_GRANT = 67043328 - 19 * 2 ** 20
+VMEM_GRANT = 67043328 - 13 * 2 ** 20
 F32 = jnp.float32
-RETURN_ORDER = ((1, 0), (3, 0), (0, 1), (0, 3), (2, 0), (0, 2), (1, 1), (3, 3), (1, 3), (3, 1),
-                (2, 1), (1, 2), (2, 3), (3, 2), (2, 2))
-
 
 def exchange_kernel(n_dev, side, n_micro, tokens, top_k, d_model, d_ff, capacity,
                     dy_hbm, yd_hbm, gate_ref, topk_ref, slot_ref, x_hbm, h1_hbm, h3_hbm, w1_hbm, w3_hbm, w2_hbm,
-                    dx_ref, dg_ref, dw1_ref, dw3_ref, dw2_ref,
-                    full, leaf, sib, dyd, dxs, ret, route, pad, w1, w3, w2, h1, h3, act_v, onehot,
+                    dx_ref, dg_ref, dw1_ref, dw3_ref, dw2_hbm,
+                    full, leaf, sib, dyd, dxs, ret, land, d2, route, pad, w1, w3, w2, h1, h3, act_v, onehot,
                     full_recv, full_send, leaf_send, sib_send, dyd_recv, route_send, route_recv,
-                    ret_send, ret_recv, load_sem, y_sem, x_sem):
+                    ret_send, ret_recv, turn_send, turn_recv, load_sem, y_sem, x_sem, d2_sem):
     me = lax.axis_index('ep')
     core = me % 2
     chip_x = (me // 2) % side
@@ -74,9 +71,7 @@
                                      full_send.at[m], full_recv.at[m, h, slot],
                                      device_id={'ep': device(da, db, core)}, device_id_type=MESH).start()
 
-    def item(m, i):
-        h = i % 2
-        ev = i // 2
+    def forward(m, h, ev):
         s = 1 - 2 * h
         k = ev % 4
         lvl = ev // 4
@@ -96,6 +91,11 @@
         def _():
             send_full(m, h, ev, 0, s, 4 + ev)
 
+    def pack(m, h, ev):
+        s = 1 - 2 * h
+        k = ev % 4
+        lvl = ev // 4
+        tok = full.at[m, h, lvl, k]
         da = (k % 2) * (1 - k // 2) * (-s) + (k // 2) * (1 - k % 2) * s + (k // 2) * (k % 2) * 2
         home = device(da, -s * lvl, core)
         leaf_chip = device(0, s * (2 * lvl - 1), 0)
@@ -127,8 +127,14 @@
         pltpu.make_async_remote_copy(sib.at[m, h, ev], target, sib_send, dyd_recv.at[m],
                                      device_id={'ep': me + 1 - 2 * core}, device_id_type=MESH).start()
 
+    def item(m, ev):
+        for h in range(2):
+            forward(m, h, ev)
+        for h in range(2):
+            pack(m, h, ev)
+
     def items(m, lo, hi):
-        lax.fori_loop(lo, hi, lambda i, c: (item(m, i), c)[1], 0)
+        lax.fori_loop(lo, hi, lambda ev, c: (item(m, ev), c)[1], 0)
 
     chunk = 256
     per_exp = (n_dev * capacity) // chunk
@@ -163,17 +169,55 @@
         h3[m, e, pl.ds(r0, chunk)] = grad_h3
         act_v[m, e, pl.ds(r0, chunk)] = act
 
+    pair_rows = 2 * capacity
+    n_turn = side * (side - 1)
+
+    def send_home(src, m, owner, dst):
+        pltpu.make_async_remote_copy(src, ret.at[m, owner], ret_send.at[m], ret_recv.at[m],
+                                     device_id={'ep': dst}, device_id_type=MESH).start()
+
     def send_return(m):
-        for which in range(2):
-            for dx, dy in RETURN_ORDER:
-                dst = (((chip_y + dy) % side) * side + (chip_x + dx) % side) * 2 + (core + which) % 2
-                send_row(m, dst)
-            if which == 0:
-                send_row(m, me + 1 - 2 * core)
-
-    def send_row(m, dst):
-        pltpu.make_async_remote_copy(own_rows(m, dst), ret.at[m, me], ret_send, ret_recv.at[m],
-                                     device_id={'ep': dst}, device_id_type=MESH).start()
+        def turn(i, carry):
+            da, db = (i // (side - 1) + 1) % side, i % (side - 1) + 1
+            chip = device(da, db, 0) // 2
+            per_blk = tokens // pair_rows
+            row0 = pl.multiple_of((chip % per_blk) * pair_rows, pair_rows)
+            pltpu.make_async_remote_copy(out_rows(m).at[:, :, chip // per_blk, pl.ds(row0, pair_rows), :], land.at[m, i],
+                                         turn_send.at[m], turn_recv.at[m, i],
+                                         device_id={'ep': device(0, db, core)}, device_id_type=MESH).start()
+            return carry
+
+        def straight(i, carry):
+            dst = device(i // 2, 0, i % 2)
+            send_home(own_rows(m, dst), m, me, dst)
+            return carry
+
+        lax.fori_loop(2, 2 * side, straight, 0)
+        lax.fori_loop(0, n_turn, turn, 0)
+        send_home(own_rows(m, me + 1 - 2 * core), m, me, me + 1 - 2 * core)
+
+    def relay(m, i):
+        da, db = (i // (side - 1) + 1) % side, i % (side - 1) + 1
+        pltpu.make_async_copy(land.at[m, i], land.at[m, i], turn_recv.at[m, i]).wait()
+        owner = device(0, -db, core)
+
+        def part(which):
+            return land.at[m, i, :, :, pl.ds(pl.multiple_of(which * capacity, capacity), capacity), :]
+
+        @pl.when(da != 0)
+        def _():
+            for which in range(2):
+                send_home(part(which), m, owner, device(da, 0, which))
+
+        @pl.when(da == 0)
+        def _():
+            send_home(part(1 - core), m, owner, me + 1 - 2 * core)
+            ret[m, owner] = part(core)[...]
+
+    def relays(m, lo, hi):
+        lax.fori_loop(lo, hi, lambda i, c: (relay(m, i), c)[1], 0)
+
+    n_home = n_dev - side
 
     def combine(m):
         pad[...] = jnp.zeros_like(pad)
@@ -185,16 +229,16 @@
             mat = jnp.where(place == key[:, j:j + 1], 1.0, mat)
         onehot[m] = mat.astype(BF16)
         ret[m, me] = own_rows(m, me)[...]
-        pltpu.make_async_copy(ret.at[m, pl.ds(0, n_dev - 1)], ret.at[m, pl.ds(0, n_dev - 1)], ret_recv.at[m]).wait()
+        pltpu.make_async_copy(ret.at[m, pl.ds(0, n_home)], ret.at[m, pl.ds(0, n_home)], ret_recv.at[m]).wait()
         for h in range(2):
             back = ret[m, :, h].reshape(n_dev * rows_dev, half)
             dx_ref[m, :, h * half:(h + 1) * half] = jnp.dot(onehot[m], back, preferred_element_type=F32).astype(BF16)
 
     pltpu.make_async_copy(route.at[pl.ds(0, n_route)], route.at[pl.ds(0, n_route)], route_recv).wait()
-    items(0, 0, 8)
-    items(1, 0, 2)
-    items(0, 8, 16)
-    items(1, 2, 8)
+    items(0, 0, 4)
+    items(1, 0, 1)
+    items(0, 4, 8)
+    items(1, 1, 4)
 
     def sent_part(m):
         return full.at[m, :, :, :, pl.ds(0, 7 * tokens // 8), :]
@@ -209,8 +253,7 @@
 
     def mixed(c, carry):
         compute(0, c)
-        item(1, 8 + 2 * c)
-        item(1, 9 + 2 * c)
+        item(1, 4 + c)
         return carry
 
     lax.fori_loop(0, 2 * per_exp, mixed, 0)
@@ -241,6 +284,12 @@
         x_copy(0, m).start()
         dy_loads[m].start()
     y_copy(0).start()
+
+    done0 = 0
+
+    def d2_copy(i):
+        col = pl.multiple_of((i % n_tile) * tile, tile)
+        return pltpu.make_async_copy(d2.at[i % 2], dw2_hbm.at[i // n_tile, :, pl.ds(col, tile)], d2_sem.at[i % 2])
 
     def weight_step(i, carry):
         @pl.when(i + 1 < 2 * n_tile)
@@ -260,10 +309,27 @@
         dy_blk = dyd[:, e, :, pl.ds(col, tile)].reshape(n_micro * rows_exp, tile)
         dw1_ref[e, pl.ds(col, tile), :] = lax.dot_general(x_blk, g1, tn, preferred_element_type=F32)
         dw3_ref[e, pl.ds(col, tile), :] = lax.dot_general(x_blk, g3, tn, preferred_element_type=F32)
-        dw2_ref[e, :, pl.ds(col, tile)] = lax.dot_general(act, dy_blk, tn, preferred_element_type=F32)
+        @pl.when(i >= 2)
+        def _():
+            d2_copy(i - 2).wait()
+
+        d2[i % 2] = lax.dot_general(act, dy_blk, tn, preferred_element_type=F32)
+        d2_copy(i).start()
+
+        @pl.when(i + done0 < n_turn)
+        def _():
+            relay(0, i + done0)
+
+        @pl.when(i + done0 >= n_turn)
+        def _():
+            relay(1, i + done0 - n_turn)
+
         return carry
 
     lax.fori_loop(0, 2 * n_tile, weight_step, 0)
+    for i in (2 * n_tile - 2, 2 * n_tile - 1):
+        d2_copy(i).wait()
+    done1 = 2 * n_tile + done0 - n_turn
     for c in dy_loads:
         c.wait()
     lane = lax.broadcasted_iota(jnp.int32, (tokens, 128), 1)
@@ -280,17 +346,24 @@
             for c in range(0, d_model, 128):
                 dy_blk = w2[0, (2 + m) * tokens:(3 + m) * tokens, c:c + 128].astype(F32)
                 part = part + dy_blk * w2[0, pl.ds(pl.multiple_of((i % 2) * tokens, tokens), tokens), c:c + 128].astype(F32)
+            @pl.when(i + done1 < n_turn - 2)
+            def _():
+                relay(1, i + done1)
+
             return jnp.where(lane == j, jnp.sum(part, axis=1, keepdims=True), total)
 
         total = lax.fori_loop(0, top_k, gate_grad, jnp.zeros((tokens, 128), F32))
         dg_ref[:, m, :] = jnp.transpose(total)[0:top_k, :]
-    for m in range(n_micro):
-        combine(m)
+    combine(0)
+    relays(1, n_turn - 2, n_turn)
+    combine(1)
     pltpu.make_async_copy(sent_part(1), sent_part(1), full_send.at[1]).wait()
     pltpu.make_async_copy(leaf, leaf, leaf_send).wait()
     pltpu.make_async_copy(sib, sib, sib_send).wait()
     pltpu.make_async_copy(route.at[pl.ds(0, n_route)], route.at[pl.ds(0, n_route)], route_send).wait()
-    pltpu.make_async_copy(ret.at[:, pl.ds(0, n_dev - 1)], ret.at[:, pl.ds(0, n_dev - 1)], ret_send).wait()
+    for m in range(n_micro):
+        pltpu.make_async_copy(ret.at[m, pl.ds(0, n_home)], ret.at[m, pl.ds(0, n_home)], ret_send.at[m]).wait()
+        pltpu.make_async_copy(land.at[m], land.at[m], turn_send.at[m]).wait()
 
 
 def solution(mesh):
@@ -324,10 +397,10 @@
                 out_vmem((top_k, n_micro, tokens), F32),
                 out_vmem(w_gate.shape, F32),
                 out_vmem(w_up.shape, F32),
-                out_vmem(w_down.shape, F32),
+                pltpu.HBM(w_down.shape, F32),
             ),
             in_specs=[hbm, hbm, vmem, vmem, vmem, hbm, hbm, hbm, hbm, hbm, hbm],
-            out_specs=(vmem,) * 5,
+            out_specs=(vmem,) * 4 + (hbm,),
             scratch_shapes=[
                 pltpu.VMEM((n_micro, 2, 2, 4, tokens, half), BF16),
                 pltpu.VMEM((n_micro, 2, 8, 2, local_exp, capacity, half), BF16),
@@ -335,6 +408,8 @@
                 pltpu.VMEM(wide_shape, BF16),
                 pltpu.VMEM((2, local_exp, rows // tokens, tokens, half), BF16),
                 pltpu.VMEM((n_micro, n_dev, 2, local_exp, capacity, half), BF16),
+                pltpu.VMEM((n_micro, side * (side - 1), 2, local_exp, 2 * capacity, half), BF16),
+                pltpu.VMEM((2, d_ff, d_ff // 2), F32),
                 pltpu.VMEM((n_dev, n_micro, 16, tokens), F32),
                 pltpu.VMEM((tokens, 128), F32),
                 pltpu.VMEM(w_gate.shape, BF16),
@@ -348,11 +423,15 @@
                 dma((n_micro,)),
                 dma, dma,
                 dma((n_micro,)),
-                dma, dma, dma,
+                dma, dma,
                 dma((n_micro,)),
+                dma((n_micro,)),
+                dma((n_micro,)),
+                dma((n_micro, side * (side - 1))),
                 dma((5,)),
                 dma((2,)),
                 dma((2, n_micro)),
+                dma((2,)),
             ],
             compiler_params=pltpu.CompilerParams(collective_id=0, has_side_effects=True, vmem_limit_bytes=VMEM_GRANT),
             cost_estimate=pl.CostEstimate(flops=10 ** 10, bytes_accessed=5 * 10 ** 7, transcendentals=0),

time: 157 us -> 143 us (0.911)
  the two profiles are of different devices: /device:TPU:125 before, /device:TPU:97 now
where the time goes in v3:
time: 143 us
  Pallas kernels  133 us (93%)
  local copies, waits for them, and re-layouts  9.77 us (7%)
    pallas_call x1, Pallas kernels, local_step(): pl.pallas_call(kernel, name='exchange', out_shape=(out_vmem((n_micro, tok...  133 us
    unnamed x9, local copies, waits for them, and re-layouts  9.77 us

profile of v3, /device:TPU:97, one launch (start us, length us, event | category | flops | bytes accessed | tf_op | source)
XLA Modules:
  0.0 143.1 jit_solution(5179195372936505554)
XLA Ops:
  0.6 132.7 %exchange.1 = (bf16[2,128,1536]{2,1,0:T(8,128)(2,1)S(1)}, f32[6,2,128]{2,1,0:T(2,128)S(1)}, f32[2,1536,512]{2,1,0:T(8,128)S(1)}, f32[2,1536,512]{2,1,0:T(8,128)S(1)}, f32[2,512,1536]{2,1,0:T(8,128)}) custom-call(bf16[2,128,1536]{2,1,0:T(8,128)(2,1)} %dy_hbm.1, bf16[2,6,128,1536]{3,2,1,0:T(8,128)(2,1)} %bitcast.8, f32[6,2,128]{2,1,0:T(2,128)} %bitcast.9, ...), custom_call_target="tpu_custom_call" | custom-call | flops 10000000000 | bytes 50000000 | tf_op jit(solution)/shard_map/exchange/pallas_call | solution.py:392
  133.4 0.0 slice-start
  133.4 0.9 copy.21
  134.2 0.6 copy.22
  134.8 0.0 slice-start.1
  134.8 2.9 %copy.23 = f32[2,1536,512]{2,1,0:T(8,128)} copy(f32[2,1536,512]{2,1,0:T(8,128)S(1)} %get-tuple-element.17) | data formatting | bytes 12582912
  137.7 2.7 %copy.24 = f32[2,1536,512]{2,1,0:T(8,128)} copy(f32[2,1536,512]{2,1,0:T(8,128)S(1)} %get-tuple-element.18) | data formatting | bytes 12582912
  140.4 0.0 slice-done
  140.4 0.0 slice-done.1
  140.4 2.7 %copy.25 = f32[2,512,1536]{2,1,0:T(8,128)} copy(f32[2,512,1536]{2,1,0:T(8,128)S(1)} %bitcast.7) | data formatting | bytes 12582912
  (1 shorter events, 0.0 us)
Async XLA Ops:
  133.4 7.1 %slice-start = ((s8[6291456]{0:T(1024)(128)(4,1)}), s8[4194304]{0:T(1024)(128)(4,1)S(1)}, s32[]{:S(2)}) async-start(s8[6291456]{0:T(1024)(128)(4,1)} %bitcast.6), calls=%async_computation | async-start | bytes 8388608
  134.8 5.6 %slice-start.1 = ((s8[6291456]{0:T(1024)(128)(4,1)}), s8[2097152]{0:T(1024)(128)(4,1)S(1)}, s32[]{:S(2)}) async-start(s8[6291456]{0:T(1024)(128)(4,1)} %bitcast.6), calls=%async_computation.1 | async-start | bytes 4194304

commit v4 on v3

--- a/solution.py
+++ b/solution.py
@@ -8,8 +8,12 @@
 
 MESH = pl.DeviceIdType.MESH
 BF16 = jnp.bfloat16
-VMEM_GRANT = 67043328 - 13 * 2 ** 20
+VMEM_GRANT = 67043328 - 13 * 2 ** 20 + 160 * 2 ** 10
 F32 = jnp.float32
+NODES = ((0, 0), (1, 0), (0, 1), (2, 0), (0, 2), (2, 3))
+EDGES = ((0, (1, 0), 1), (0, (0, 1), 2), (1, (1, 0), 3), (2, (0, 1), 4), (3, (0, -1), 5))
+LEAVES = (((-1, 0), (0, -1)), ((0, 1), (0, -1)), ((-1, 0), (-1, 0)), ((0, 1), (0, 1)), ((1, 0), (-1, 0)), ((0, -1), (1, 0)))
+
 
 def exchange_kernel(n_dev, side, n_micro, tokens, top_k, d_model, d_ff, capacity,
                     dy_hbm, yd_hbm, gate_ref, topk_ref, slot_ref, x_hbm, h1_hbm, h3_hbm, w1_hbm, w3_hbm, w2_hbm,
@@ -61,8 +65,7 @@
                                      device_id={'ep': device(da, db, core)}, device_id_type=MESH).start()
 
     n_route = 0
-    for da, db in ((1, 0), (side - 1, 0), (2, 0), (0, 1), (0, side - 1), (1, 1), (1, side - 1), (side - 1, 1),
-                   (side - 1, side - 1), (2, 1), (2, side - 1)):
+    for da, db in sorted({(q * a % side, q * b % side) for a, b in NODES[1:] for q in (1, -1)}):
         send_route(da, db)
         n_route += 1
 
@@ -73,41 +76,34 @@
 
     def forward(m, h, ev):
         s = 1 - 2 * h
-        k = ev % 4
-        lvl = ev // 4
-        tok = full.at[m, h, lvl, k]
+        tok = full.at[m, h, ev // 4, ev % 4]
         pltpu.make_async_copy(tok, tok, full_recv.at[m, h, ev]).wait()
-
-        @pl.when(ev == 0)
-        def _():
-            send_full(m, h, ev, s, 0, 1)
-            send_full(m, h, ev, -s, 0, 2)
-
-        @pl.when(ev == 1)
-        def _():
-            send_full(m, h, ev, s, 0, 3)
-
-        @pl.when(ev < 4)
-        def _():
-            send_full(m, h, ev, 0, s, 4 + ev)
+        for src, (da, db), slot in EDGES:
+            @pl.when(ev == src)
+            def _(da=da, db=db, slot=slot):
+                send_full(m, h, ev, s * da, s * db, slot)
+
+    def by_event(ev, values):
+        out = values[0]
+        for i, v in enumerate(values[1:]):
+            out = jnp.where(ev == i + 1, v, out)
+        return out
 
     def pack(m, h, ev):
         s = 1 - 2 * h
-        k = ev % 4
-        lvl = ev // 4
-        tok = full.at[m, h, lvl, k]
-        da = (k % 2) * (1 - k // 2) * (-s) + (k // 2) * (1 - k % 2) * s + (k // 2) * (k % 2) * 2
-        home = device(da, -s * lvl, core)
-        leaf_chip = device(0, s * (2 * lvl - 1), 0)
-        row = lax.broadcasted_iota(jnp.int32, (4 * rows_dev, tokens), 0)
+        tok = full.at[m, h, ev // 4, ev % 4]
+        home = device(-s * by_event(ev, [p[0] for p in NODES]), -s * by_event(ev, [p[1] for p in NODES]), core)
+        leaf_chip = [device(s * by_event(ev, [p[i][0] for p in LEAVES]), s * by_event(ev, [p[i][1] for p in LEAVES]), 0)
+                     for i in range(2)]
+        row = lax.broadcasted_iota(jnp.int32, (6 * rows_dev, tokens), 0)
         block = row // rows_dev
         inner = row - block * rows_dev
-        dev = jnp.where(block == 0, me, jnp.where(block == 1, me + 1 - 2 * core,
-                                                  jnp.where(block == 2, leaf_chip, leaf_chip + 1)))
+        dev = jnp.where(block < 4, leaf_chip[0] + block - 2, leaf_chip[1] + block - 4)
+        dev = jnp.where(block == 0, me, jnp.where(block == 1, me + 1 - 2 * core, dev))
         want = (dev * rows_dev + inner).astype(F32)
         table = route[home, m]
-        pick = jnp.zeros((4 * rows_dev, tokens), F32)
-        gate = jnp.zeros((4 * rows_dev, tokens), F32)
+        pick = jnp.zeros((6 * rows_dev, tokens), F32)
+        gate = jnp.zeros((6 * rows_dev, tokens), F32)
         for j in range(top_k):
             hit = want == table[j:j + 1, :]
             pick = jnp.where(hit, 1.0, pick)
@@ -115,15 +111,24 @@
         gate = jnp.sum(gate, axis=1, keepdims=True)
         rows = jnp.dot(pick.astype(BF16), tok[...], preferred_element_type=F32)
         rows = (rows * gate).astype(BF16)
-        leaf[m, h, ev] = rows[2 * rows_dev:].reshape(2, 2, capacity, half)
+        leaf[m, h, ev] = rows[2 * rows_dev:].reshape(2, 2, 2, capacity, half)
         sib[m, h, ev] = rows[rows_dev:2 * rows_dev].reshape(2, capacity, half)
         row0 = pl.multiple_of(home * capacity, capacity)
         col0 = pl.multiple_of(h * half, half)
         dyd[m, :, pl.ds(row0, capacity), pl.ds(col0, half)] = rows[:rows_dev].reshape(2, capacity, half)
         target = dyd.at[m, :, pl.ds(row0, capacity), pl.ds(col0, half)]
-        for c in range(2):
-            pltpu.make_async_remote_copy(leaf.at[m, h, ev, c], target, leaf_send, dyd_recv.at[m],
-                                         device_id={'ep': leaf_chip + c}, device_id_type=MESH).start()
+
+        def send_leaf(i):
+            for c in range(2):
+                pltpu.make_async_remote_copy(leaf.at[m, h, ev, i, c], target, leaf_send, dyd_recv.at[m],
+                                             device_id={'ep': leaf_chip[i] + c}, device_id_type=MESH).start()
+
+        send_leaf(0)
+
+        @pl.when(by_event(ev, [int(len(set(p)) == 2) for p in LEAVES]) == 1)
+        def _():
+            send_leaf(1)
+
         pltpu.make_async_remote_copy(sib.at[m, h, ev], target, sib_send, dyd_recv.at[m],
                                      device_id={'ep': me + 1 - 2 * core}, device_id_type=MESH).start()
 
@@ -227,24 +232,26 @@
         mat = jnp.zeros((tokens, n_dev * rows_dev), F32)
         for j in range(top_k):
             mat = jnp.where(place == key[:, j:j + 1], 1.0, mat)
-        onehot[m] = mat.astype(BF16)
+        onehot[...] = mat.astype(BF16)
         ret[m, me] = own_rows(m, me)[...]
         pltpu.make_async_copy(ret.at[m, pl.ds(0, n_home)], ret.at[m, pl.ds(0, n_home)], ret_recv.at[m]).wait()
         for h in range(2):
-            back = ret[m, :, h].reshape(n_dev * rows_dev, half)
-            dx_ref[m, :, h * half:(h + 1) * half] = jnp.dot(onehot[m], back, preferred_element_type=F32).astype(BF16)
+            for c in range(0, half, 256):
+                back = ret[m, :, h, :, :, c:c + 256].reshape(n_dev * rows_dev, 256)
+                dx_ref[m, :, h * half + c:h * half + c + 256] = jnp.dot(
+                    onehot[...], back, preferred_element_type=F32).astype(BF16)
 
     pltpu.make_async_copy(route.at[pl.ds(0, n_route)], route.at[pl.ds(0, n_route)], route_recv).wait()
-    items(0, 0, 4)
+    items(0, 0, 3)
     items(1, 0, 1)
-    items(0, 4, 8)
-    items(1, 1, 4)
+    items(0, 3, 6)
+    items(1, 1, 2)
 
     def sent_part(m):
-        return full.at[m, :, :, :, pl.ds(0, 7 * tokens // 8), :]
+        return full.at[m, :, :, :, pl.ds(0, len(EDGES) * tokens // 8), :]
 
     def wait_dyd(m):
-        part = dyd.at[m, :, pl.ds(0, (n_dev - 8) * capacity)]
+        part = dyd.at[m, :, pl.ds(0, (n_dev - len(NODES)) * capacity)]
         pltpu.make_async_copy(part, part, dyd_recv.at[m]).wait()
 
     for c in loads:
@@ -253,7 +260,7 @@
 
     def mixed(c, carry):
         compute(0, c)
-        item(1, 4 + c)
+        item(1, 2 + c)
         return carry
 
     lax.fori_loop(0, 2 * per_exp, mixed, 0)
@@ -289,7 +296,7 @@
 
     def d2_copy(i):
         col = pl.multiple_of((i % n_tile) * tile, tile)
-        return pltpu.make_async_copy(d2.at[i % 2], dw2_hbm.at[i // n_tile, :, pl.ds(col, tile)], d2_sem.at[i % 2])
+        return pltpu.make_async_copy(d2.at[0], dw2_hbm.at[i // n_tile, :, pl.ds(col, tile)], d2_sem.at[0])
 
     def weight_step(i, carry):
         @pl.when(i + 1 < 2 * n_tile)
@@ -309,11 +316,11 @@
         dy_blk = dyd[:, e, :, pl.ds(col, tile)].reshape(n_micro * rows_exp, tile)
         dw1_ref[e, pl.ds(col, tile), :] = lax.dot_general(x_blk, g1, tn, preferred_element_type=F32)
         dw3_ref[e, pl.ds(col, tile), :] = lax.dot_general(x_blk, g3, tn, preferred_element_type=F32)
-        @pl.when(i >= 2)
-        def _():
-            d2_copy(i - 2).wait()
-
-        d2[i % 2] = lax.dot_general(act, dy_blk, tn, preferred_element_type=F32)
+        @pl.when(i >= 1)
+        def _():
+            d2_copy(i - 1).wait()
+
+        d2[0] = lax.dot_general(act, dy_blk, tn, preferred_element_type=F32)
         d2_copy(i).start()
 
         @pl.when(i + done0 < n_turn)
@@ -327,8 +334,7 @@
         return carry
 
     lax.fori_loop(0, 2 * n_tile, weight_step, 0)
-    for i in (2 * n_tile - 2, 2 * n_tile - 1):
-        d2_copy(i).wait()
+    d2_copy(2 * n_tile - 1).wait()
     done1 = 2 * n_tile + done0 - n_turn
     for c in dy_loads:
         c.wait()
@@ -358,7 +364,9 @@
     relays(1, n_turn - 2, n_turn)
     combine(1)
     pltpu.make_async_copy(sent_part(1), sent_part(1), full_send.at[1]).wait()
-    pltpu.make_async_copy(leaf, leaf, leaf_send).wait()
+    n_leaf = sum(len(set(p)) for p in LEAVES)
+    part = leaf.at[:, :, pl.ds(0, n_leaf // 2)]
+    pltpu.make_async_copy(part, part, leaf_send).wait()
     pltpu.make_async_copy(sib, sib, sib_send).wait()
     pltpu.make_async_copy(route.at[pl.ds(0, n_route)], route.at[pl.ds(0, n_route)], route_send).wait()
     for m in range(n_micro):
@@ -403,13 +411,13 @@
             out_specs=(vmem,) * 4 + (hbm,),
             scratch_shapes=[
                 pltpu.VMEM((n_micro, 2, 2, 4, tokens, half), BF16),
-                pltpu.VMEM((n_micro, 2, 8, 2, local_exp, capacity, half), BF16),
-                pltpu.VMEM((n_micro, 2, 8, local_exp, capacity, half), BF16),
+                pltpu.VMEM((n_micro, 2, len(NODES), 2, 2, local_exp, capacity, half), BF16),
+                pltpu.VMEM((n_micro, 2, len(NODES), local_exp, capacity, half), BF16),
                 pltpu.VMEM(wide_shape, BF16),
                 pltpu.VMEM((2, local_exp, rows // tokens, tokens, half), BF16),
                 pltpu.VMEM((n_micro, n_dev, 2, local_exp, capacity, half), BF16),
                 pltpu.VMEM((n_micro, side * (side - 1), 2, local_exp, 2 * capacity, half), BF16),
-                pltpu.VMEM((2, d_ff, d_ff // 2), F32),
+                pltpu.VMEM((1, d_ff, d_ff // 2), F32),
                 pltpu.VMEM((n_dev, n_micro, 16, tokens), F32),
                 pltpu.VMEM((tokens, 128), F32),
                 pltpu.VMEM(w_gate.shape, BF16),
@@ -418,7 +426,7 @@
                 pltpu.VMEM(ff_shape, BF16),
                 pltpu.VMEM(ff_shape, BF16),
                 pltpu.VMEM(ff_shape, BF16),
-                pltpu.VMEM((n_micro, tokens, n_dev * local_exp * capacity), BF16),
+                pltpu.VMEM((tokens, n_dev * local_exp * capacity), BF16),
                 dma((n_micro, 2, 8)),
                 dma((n_micro,)),
                 dma, dma,

time: 143 us -> 140 us (0.979)
  Pallas kernels: 133 us -> 130 us
    pallas_call x1, Pallas kernels: 133 us -> 130 us  [local_step(): pl.pallas_call(kernel, name='exchange', out_shape=(out_vmem((n_micro, tok...]
where the time goes in v4:
time: 140 us
  Pallas kernels  130 us (93%)
  local copies, waits for them, and re-layouts  9.77 us (7%)
    pallas_call x1, Pallas kernels, local_step(): pl.pallas_call(kernel, name='exchange', out_shape=(out_vmem((n_micro, tok...  130 us
    unnamed x9, local copies, waits for them, and re-layouts  9.77 us

profile of v4, /device:TPU:97, one launch (start us, length us, event | category | flops | bytes accessed | tf_op | source)
XLA Modules:
  0.0 140.2 jit_solution(14986201826615074300)
XLA Ops:
  0.6 129.7 %exchange.1 = (bf16[2,128,1536]{2,1,0:T(8,128)(2,1)S(1)}, f32[6,2,128]{2,1,0:T(2,128)S(1)}, f32[2,1536,512]{2,1,0:T(8,128)S(1)}, f32[2,1536,512]{2,1,0:T(8,128)S(1)}, f32[2,512,1536]{2,1,0:T(8,128)}) custom-call(bf16[2,128,1536]{2,1,0:T(8,128)(2,1)} %dy_hbm.1, bf16[2,6,128,1536]{3,2,1,0:T(8,128)(2,1)} %bitcast.8, f32[6,2,128]{2,1,0:T(2,128)} %bitcast.9, ...), custom_call_target="tpu_custom_call" | custom-call | flops 10000000000 | bytes 50000000 | tf_op jit(solution)/shard_map/exchange/pallas_call | solution.py:400
  130.4 0.0 slice-start
  130.4 0.9 copy.21
  131.3 0.6 copy.22
  131.8 0.0 slice-start.1
  131.9 2.9 %copy.23 = f32[2,1536,512]{2,1,0:T(8,128)} copy(f32[2,1536,512]{2,1,0:T(8,128)S(1)} %get-tuple-element.17) | data formatting | bytes 12582912
  134.7 2.7 %copy.24 = f32[2,1536,512]{2,1,0:T(8,128)} copy(f32[2,1536,512]{2,1,0:T(8,128)S(1)} %get-tuple-element.18) | data formatting | bytes 12582912
  137.4 0.0 slice-done
  137.4 0.0 slice-done.1
  137.4 2.7 %copy.25 = f32[2,512,1536]{2,1,0:T(8,128)} copy(f32[2,512,1536]{2,1,0:T(8,128)S(1)} %bitcast.7) | data formatting | bytes 12582912
  (1 shorter events, 0.0 us)
Async XLA Ops:
  130.4 7.1 %slice-start = ((s8[6291456]{0:T(1024)(128)(4,1)}), s8[4194304]{0:T(1024)(128)(4,1)S(1)}, s32[]{:S(2)}) async-start(s8[6291456]{0:T(1024)(128)(4,1)} %bitcast.6), calls=%async_computation | async-start | bytes 8388608
  131.8 5.6 %slice-start.1 = ((s8[6291456]{0:T(1024)(128)(4,1)}), s8[2097152]{0:T(1024)(128)(4,1)S(1)}, s32[]{:S(2)}) async-start(s8[6291456]{0:T(1024)(128)(4,1)} %bitcast.6), calls=%async_computation.1 | async-start | bytes 4194304

commit v5 on v4

--- a/solution.py
+++ b/solution.py
@@ -242,9 +242,9 @@
                     onehot[...], back, preferred_element_type=F32).astype(BF16)
 
     pltpu.make_async_copy(route.at[pl.ds(0, n_route)], route.at[pl.ds(0, n_route)], route_recv).wait()
-    items(0, 0, 3)
+    items(0, 0, 1)
     items(1, 0, 1)
-    items(0, 3, 6)
+    items(0, 1, 6)
     items(1, 1, 2)
 
     def sent_part(m):
@@ -374,6 +374,27 @@
         pltpu.make_async_copy(land.at[m], land.at[m], turn_send.at[m]).wait()
 
 
+def finish_kernel(dx_ref, dg_ref, dw1_ref, dw3_ref, dx_out, dg_out, dw1_out, dw3_out, sem):
+    copies = [pltpu.make_async_copy(src, dst, sem.at[i]) for i, (src, dst) in enumerate(
+        ((dw1_ref, dw1_out), (dw3_ref, dw3_out), (dx_ref, dx_out), (dg_ref, dg_out)))]
+    for c in copies:
+        c.start()
+    for c in copies:
+        c.wait()
+
+
+def finish(results):
+    return pl.pallas_call(
+        finish_kernel,
+        name='finish',
+        out_shape=tuple(jax.ShapeDtypeStruct(r.shape, r.dtype) for r in results),
+        in_specs=[pl.BlockSpec(memory_space=pltpu.VMEM)] * 4,
+        out_specs=(pl.BlockSpec(memory_space=pl.ANY),) * 4,
+        scratch_shapes=[pltpu.SemaphoreType.DMA((4,))],
+        compiler_params=pltpu.CompilerParams(vmem_limit_bytes=2 ** 20),
+    )(*results)
+
+
 def solution(mesh):
     n_dev = mesh.shape['ep']
     side = 1
@@ -397,7 +418,7 @@
         ff_shape = (n_micro, local_exp, rows, d_ff)
         wide_shape = (n_micro, local_exp, rows, d_model)
         out_vmem = pltpu.VMEM
-        grad_x, grad_gate, grad_w_gate, grad_w_up, grad_w_down = pl.pallas_call(
+        *results, grad_w_down = pl.pallas_call(
             kernel,
             name='exchange',
             out_shape=(
@@ -445,6 +466,7 @@
             cost_estimate=pl.CostEstimate(flops=10 ** 10, bytes_accessed=5 * 10 ** 7, transcendentals=0),
         )(grad_out, jnp.transpose(expert_out, (0, 2, 1, 3)), by_choice(gate_vals), by_choice(topk_idx), by_choice(slot_idx),
           x_dispatch, h1_pre, h3_pre, w_gate, w_up, w_down)
+        grad_x, grad_gate, grad_w_gate, grad_w_up = finish(results)
         grad_gate = jnp.transpose(grad_gate, (1, 2, 0))
         return grad_x, grad_gate, grad_w_gate, grad_w_up, grad_w_down
 

time: 140 us -> 140 us (level)
  local copies, waits for them, and re-layouts: 9.77 us -> 3.34 us
  Pallas kernels: 130 us -> 136 us
    pallas_call x0 -> x1, Pallas kernels: none -> 6.44 us  [finish(): pl.pallas_call(finish_kernel, name='finish', out_shape=tuple((jax.ShapeDt...]
    unnamed x9 -> x3, local copies, waits for them, and re-layouts: 9.77 us -> 3.34 us
where the time goes in v5:
time: 140 us
  Pallas kernels  136 us (97%)
  local copies, waits for them, and re-layouts  3.34 us (2%)
    pallas_call x1, Pallas kernels, local_step(): pl.pallas_call(kernel, name='exchange', out_shape=(out_vmem((n_micro, tok...  129 us
    pallas_call x1, Pallas kernels, finish(): pl.pallas_call(finish_kernel, name='finish', out_shape=tuple((jax.ShapeDt...  6.44 us
    unnamed x3, local copies, waits for them, and re-layouts  3.34 us

profile of v5, /device:TPU:97, one launch (start us, length us, event | category | flops | bytes accessed | tf_op | source)
XLA Modules:
  0.0 139.8 jit_solution(13046197664750352474)
XLA Ops:
  0.6 129.4 %exchange.1 = (bf16[2,128,1536]{2,1,0:T(8,128)(2,1)S(1)}, f32[6,2,128]{2,1,0:T(2,128)S(1)}, f32[2,1536,512]{2,1,0:T(8,128)S(1)}, f32[2,1536,512]{2,1,0:T(8,128)S(1)}, f32[2,512,1536]{2,1,0:T(8,128)}) custom-call(bf16[2,128,1536]{2,1,0:T(8,128)(2,1)} %dy_hbm.1, bf16[2,6,128,1536]{3,2,1,0:T(8,128)(2,1)} %bitcast.5, f32[6,2,128]{2,1,0:T(2,128)} %bitcast.6, ...), custom_call_target="tpu_custom_call" | custom-call | flops 10000000000 | bytes 50000000 | tf_op jit(solution)/shard_map/exchange/pallas_call | solution.py:421
  130.1 0.0 copy-start
  130.1 6.4 %finish.1 = (bf16[2,128,1536]{2,1,0:T(8,128)(2,1)}, f32[6,2,128]{2,1,0:T(2,128)}, f32[2,1536,512]{2,1,0:T(8,128)}, f32[2,1536,512]{2,1,0:T(8,128)}) custom-call(bf16[2,128,1536]{2,1,0:T(8,128)(2,1)S(1)} %get-tuple-element.14.dx_ref, f32[6,2,128]{2,1,0:T(2,128)S(1)} %get-tuple-element.15.dg_ref, f32[2,1536,512]{2,1,0:T(8,128)S(1)} %get-tuple-element.16.dw1_ref, ...), custom_call_target="tpu_custom_call" | custom-call | tf_op jit(solution)/shard_map/finish/pallas_call | solution.py:387
  136.5 0.6 copy-done
  137.1 2.7 %copy.17 = f32[2,512,1536]{2,1,0:T(8,128)} copy(f32[2,512,1536]{2,1,0:T(8,128)S(1)} %copy-done) | data formatting | bytes 12582912
Async XLA Ops:
  130.1 7.1 %copy-start = (f32[2,512,1536]{2,1,0:T(8,128)S(1)}, f32[2,512,1536]{2,1,0:T(8,128)}, u32[]{:S(2)}) copy-start(f32[2,512,1536]{2,1,0:T(8,128)} %get-tuple-element.32) | copy-start | bytes 18874372
